TPU v7x, 32 devices: a whole 2x2x4 slice. The times are simulated.
32 devices in a mesh: vocab: 8 (over y, x, core), dp: 4 (over z).
Axes of the slice: x: 2, y: 2, z: 4, core: 2. Of those that a mesh axis runs over, the one named last changes fastest.
Arguments:
- token_ids: int32 [8192], P(('vocab', 'dp')), may hold values from 0 to 50256
- target_ids: int32 [8192], P(('vocab', 'dp')), may hold values from 0 to 50256
- loss_mask: int32 [8192], P(('vocab', 'dp')), may hold values from 0 to 1, as said below
- seq_ids: int32 [8192], P(('vocab', 'dp')), may hold values from 0 to 255, as said below
- embed_table: bfloat16 [50304, 1024], P('vocab'), may hold values from -0.359375 to 0.359375
- pos_table: bfloat16 [1024, 1024], replicated, may hold values from -0.359375 to 0.359375
- gains: float32 [3, 1024], replicated, may hold values from 0.5 to 1.5
- shifts: float32 [3, 1024], replicated, may hold values from -1.8 to 1.8
- linear_bias: float32 [1, 9216], replicated, may hold values from -1.8 to 1.8
- query_key_value_weight: bfloat16 [1, 1024, 3072], replicated, may hold values from -0.1875 to 0.1875
- w_out: bfloat16 [1, 1024, 1024], replicated, may hold values from -0.5 to 0.5
- w_fc: bfloat16 [1, 1024, 4096], replicated, may hold values from -0.1875 to 0.1875
- w_proj: bfloat16 [1, 4096, 1024], replicated, may hold values from -0.09375 to 0.09375
- adapters: float32 [1, 24576], P(None, 'vocab'), may hold values from -0.18 to 0.18
- first_moment: float32 [1, 24576], P(None, 'vocab'), may hold values from -4.2483338e-05 to 4.2483338e-05
- second_moment: float32 [1, 24576], P(None, 'vocab'), may hold values from 2.0345052e-12 to 3.2552083e-11
- step_count: int32 [1], replicated, may hold values from 2 to 20
Outputs:
- loss: float32 [], replicated
- grad_norm: float32 [], replicated
- new_adapters: float32 [1, 24576], P(None, 'vocab')
- new_first: float32 [1, 24576], P(None, 'vocab')
- new_second: float32 [1, 24576], P(None, 'vocab')
- adapter_copy: bfloat16 [1, 24576], P(None, 'vocab')
Inputs may be any that keep to these rules, and one draw needn't show every extreme that they name: seq_ids never falls; the tokens of each device form whole sequences of 256 // 8 times 1, 2, 4 or 8 tokens, each starting at a multiple of its length within the device; some device holds one sequence of 256 tokens and some device eight of 32. `token_ids`: every id is a real row, below 50257. `target_ids`: every target is a real row, below 50257. `loss_mask`: the share of ones differs from device to device; some devices have all ones.
All inputs are finite; a program needn't handle non-finite values.
Results may differ from a plain program's by a relative error of at most 0.0051.
Values may be sent and summed in bfloat16 or wider, within the bound.
A program may use at most 256 MiB of HBM per device.

v0:
```python
import jax
import jax.numpy as jnp
from jax import lax
from jax.sharding import PartitionSpec as P

MODEL_WIDTH = 1024
HEADS = 16
HEAD_DIM = 64
FF = 4096
VOCAB_REAL = 50257
RANK = 4
LAYERS = 1
TOK_DEV = 256
PRECISE = lax.Precision.HIGHEST
ADAPTER_SCALE = 8.0
CLIP_NORM = 0.01
BETA_ONE = 0.9
BETA_TWO = 0.999
ADAM_EPS = 1e-08
WEIGHT_DECAY = 0.01
LEARN_RATE = 0.02


def mixed_product(left, right):
    return jnp.dot(left, right, preferred_element_type=jnp.float32)


def exact_product(left, right):
    return jnp.dot(left.astype(jnp.float32), right.astype(jnp.float32), precision=PRECISE)


def layer_norm(values, gain, shift):
    center = values - jnp.mean(values, -1, keepdims=True)
    spread = jnp.mean(center * center, -1, keepdims=True)
    inverse = lax.rsqrt(spread + 1e-05)
    normed = center * inverse
    return (normed * gain + shift, normed, inverse)


def norm_back(grad_in, normed, inverse, gain):
    scaled = grad_in * gain
    return inverse * (
        scaled
        - jnp.mean(scaled, -1, keepdims=True)
        - normed * jnp.mean(scaled * normed, -1, keepdims=True)
    )


def gelu(values):
    return (
        0.5
        * values
        * (1.0 + jnp.tanh(0.7978845608028654 * (values + 0.044715 * values * values * values)))
    )


def positions_of(seq):
    place = jnp.arange(seq.shape[0], dtype=jnp.int32)
    fresh = jnp.concatenate([jnp.ones((1,), bool), seq[1:] != seq[:-1]])
    start = lax.cummax(jnp.where(fresh, place, 0))
    return place - start


def split_adapter(flat):
    width = MODEL_WIDTH * RANK
    qkv_down_matrix = flat[:width].reshape(MODEL_WIDTH, RANK)
    output_down_matrix = flat[width : 2 * width].reshape(MODEL_WIDTH, RANK)
    qkv_up_matrix = flat[2 * width : 5 * width].reshape(RANK, 3 * MODEL_WIDTH)
    output_up_matrix = flat[5 * width :].reshape(RANK, MODEL_WIDTH)
    return (qkv_down_matrix, output_down_matrix, qkv_up_matrix, output_up_matrix)


def split_heads(query_key_value):
    count = query_key_value.shape[0]
    query = query_key_value[:, :MODEL_WIDTH].reshape(count, HEADS, HEAD_DIM)
    keys = query_key_value[:, MODEL_WIDTH : 2 * MODEL_WIDTH].reshape(count, HEADS, HEAD_DIM)
    values = query_key_value[:, 2 * MODEL_WIDTH :].reshape(count, HEADS, HEAD_DIM)
    return (query, keys, values)


def attention_forward(query_key_value, visible):
    query, keys, values = split_heads(query_key_value)
    scores = jnp.einsum("qhd,khd->hqk", query, keys, preferred_element_type=jnp.float32) * 0.125
    scores = jnp.where(visible[None], scores, -1e30)
    row_top = jnp.max(scores, -1, keepdims=True)
    expd = jnp.exp(scores - row_top)
    row_total = jnp.sum(expd, -1, keepdims=True)
    probs = (expd / row_total).astype(jnp.bfloat16)
    attention_output = jnp.einsum("hqk,khd->qhd", probs, values, preferred_element_type=jnp.float32)
    return (
        attention_output.reshape(query_key_value.shape[0], MODEL_WIDTH),
        row_top + jnp.log(row_total),
    )


def attention_back(query_key_value, visible, row_lse, attention_output_gradient):
    query, keys, values = split_heads(query_key_value)
    count = query_key_value.shape[0]
    scores = jnp.einsum("qhd,khd->hqk", query, keys, preferred_element_type=jnp.float32) * 0.125
    probs = jnp.where(visible[None], jnp.exp(scores - row_lse), 0.0)
    grad_heads = attention_output_gradient.reshape(count, HEADS, HEAD_DIM)
    grad_probs = jnp.einsum("qhd,khd->hqk", grad_heads, values, preferred_element_type=jnp.float32)
    grad_values = jnp.einsum(
        "hqk,qhd->khd", probs.astype(jnp.bfloat16), grad_heads, preferred_element_type=jnp.float32
    )
    grad_scores = probs * (grad_probs - jnp.sum(probs * grad_probs, -1, keepdims=True))
    grad_scores = grad_scores.astype(jnp.bfloat16)
    grad_query = (
        jnp.einsum("hqk,khd->qhd", grad_scores, keys, preferred_element_type=jnp.float32) * 0.125
    )
    grad_keys = (
        jnp.einsum("hqk,qhd->khd", grad_scores, query, preferred_element_type=jnp.float32) * 0.125
    )
    joined = jnp.concatenate(
        [
            grad_query.reshape(count, MODEL_WIDTH),
            grad_keys.reshape(count, MODEL_WIDTH),
            grad_values.reshape(count, MODEL_WIDTH),
        ],
        axis=1,
    )
    return joined.astype(jnp.bfloat16)


def local(
    token_ids,
    target_ids,
    loss_mask,
    seq_ids,
    embed_table,
    pos_table,
    gains,
    shifts,
    linear_bias,
    query_key_value_weight,
    w_out,
    w_fc,
    w_proj,
    adapters,
    first_moment,
    second_moment,
    step_count,
):
    vocab_place = lax.axis_index("vocab")
    vocab_count = lax.axis_size("vocab")
    total_tokens = TOK_DEV * vocab_count * lax.axis_size("dp")
    shard_rows = embed_table.shape[0]
    all_tokens, all_targets, all_mask = (
        lax.all_gather(token_ids, "vocab", axis=0, tiled=True),
        lax.all_gather(target_ids, "vocab", axis=0, tiled=True),
        lax.all_gather(loss_mask, "vocab", axis=0, tiled=True),
    )
    mask_weights = all_mask.astype(jnp.float32)
    wanted = all_tokens - vocab_place * shard_rows
    inside = (wanted >= 0) & (wanted < shard_rows)
    picked_rows = jnp.take(embed_table, jnp.clip(wanted, 0, shard_rows - 1), axis=0)
    embedded = lax.psum_scatter(
        jnp.where(inside[:, None], picked_rows.astype(jnp.float32), 0.0).astype(jnp.bfloat16),
        "vocab",
        scatter_dimension=0,
        tiled=True,
    ).astype(jnp.float32)
    copies = lax.all_gather(adapters.astype(jnp.bfloat16), "vocab", axis=1, tiled=True)
    resid = embedded + pos_table[positions_of(seq_ids)].astype(jnp.float32)
    place = jnp.arange(TOK_DEV)
    visible = (seq_ids[:, None] == seq_ids[None, :]) & (place[None, :] <= place[:, None])
    layer_params = 0
    qkv_down_matrix, output_down_matrix, qkv_up_matrix, output_up_matrix = split_adapter(
        copies[layer_params]
    )
    bias_vector = linear_bias[layer_params]
    hidden_first, normed_one, inverse_one = layer_norm(
        resid, gains[2 * layer_params], shifts[2 * layer_params]
    )
    hidden_first = hidden_first.astype(jnp.bfloat16)
    adapter_input = mixed_product(hidden_first, qkv_down_matrix).astype(jnp.bfloat16)
    query_key_value = (
        mixed_product(hidden_first, query_key_value_weight[layer_params])
        + bias_vector[: 3 * MODEL_WIDTH]
        + ADAPTER_SCALE * mixed_product(adapter_input, qkv_up_matrix)
    )
    query_key_value = query_key_value.astype(jnp.bfloat16)
    attention_output, row_lse = attention_forward(query_key_value, visible)
    attention_output = attention_output.astype(jnp.bfloat16)
    adapter_middle = mixed_product(attention_output, output_down_matrix).astype(jnp.bfloat16)
    resid = (
        resid
        + mixed_product(attention_output, w_out[layer_params])
        + bias_vector[3 * MODEL_WIDTH : 4 * MODEL_WIDTH]
        + ADAPTER_SCALE * mixed_product(adapter_middle, output_up_matrix)
    )
    h_two, normed_two, inverse_two = layer_norm(
        resid, gains[2 * layer_params + 1], shifts[2 * layer_params + 1]
    )
    h_two = h_two.astype(jnp.bfloat16)
    pre = (
        mixed_product(h_two, w_fc[layer_params])
        + bias_vector[4 * MODEL_WIDTH : 4 * MODEL_WIDTH + FF]
    )
    act = gelu(pre).astype(jnp.bfloat16)
    resid = resid + mixed_product(act, w_proj[layer_params]) + bias_vector[4 * MODEL_WIDTH + FF :]
    saved = [
        (
            hidden_first,
            normed_one,
            inverse_one,
            adapter_input,
            query_key_value,
            row_lse,
            attention_output,
            adapter_middle,
            normed_two,
            inverse_two,
            pre,
        )
    ]
    hidden, normed_last, inverse_last = layer_norm(resid, gains[2 * LAYERS], shifts[2 * LAYERS])
    hidden = hidden.astype(jnp.bfloat16)
    columns = vocab_place * shard_rows + jnp.arange(shard_rows)
    live = columns < VOCAB_REAL

    def head_logits(row_block):
        logits = jnp.einsum("td,vd->tv", row_block, embed_table, preferred_element_type=jnp.float32)
        return jnp.where(live[None], logits, -1e30)

    piece = lax.all_gather(hidden, "vocab", axis=0, tiled=True)
    logits = head_logits(piece)
    row_top = jnp.max(logits, -1)
    row_total = jnp.sum(jnp.exp(logits - row_top[:, None]), -1)
    wanted = all_targets
    picked = jnp.sum(jnp.where(columns[None, :] == wanted[:, None], logits, 0.0), -1)
    gathered, row_top, row_total, picked = (piece, row_top, row_total, picked)
    joint_top = lax.pmax(row_top, "vocab")
    row_total = row_total * jnp.exp(row_top - joint_top)
    row_total, picked = lax.psum((row_total, picked), "vocab")
    row_lse = joint_top + jnp.log(row_total)
    loss_part = jnp.sum(mask_weights * (row_lse - picked))
    row_block = gathered
    logits = head_logits(row_block)
    wanted = all_targets
    hit = (columns[None, :] == wanted[:, None]).astype(jnp.float32)
    grad_logits = (
        mask_weights[:, None] * (jnp.exp(logits - row_lse[:, None]) - hit) * (1.0 / total_tokens)
    ).astype(jnp.bfloat16)
    grad_hidden = lax.psum_scatter(
        mixed_product(grad_logits, embed_table), "vocab", scatter_dimension=0, tiled=True
    )
    grad_resid = norm_back(grad_hidden, normed_last, inverse_last, gains[2 * LAYERS])
    layer_grads = []
    for layer_params in reversed(range(LAYERS)):
        (
            hidden_first,
            normed_one,
            inverse_one,
            adapter_input,
            query_key_value,
            row_lse_l,
            attention_output,
            adapter_middle,
            normed_two,
            inverse_two,
            pre,
        ) = saved[layer_params]
        qkv_down_matrix, output_down_matrix, qkv_up_matrix, output_up_matrix = split_adapter(
            copies[layer_params]
        )
        grad_top = grad_resid.astype(jnp.bfloat16)
        grad_act = jnp.einsum(
            "te,fe->tf", grad_top, w_proj[layer_params], preferred_element_type=jnp.float32
        )
        grad_pre = jax.vjp(gelu, pre)[1](grad_act)[0].astype(jnp.bfloat16)
        grad_h_two = jnp.einsum(
            "tf,df->td", grad_pre, w_fc[layer_params], preferred_element_type=jnp.float32
        )
        grad_resid = grad_resid + norm_back(
            grad_h_two, normed_two, inverse_two, gains[2 * layer_params + 1]
        )
        middle_gradient = grad_resid.astype(jnp.bfloat16)
        adapter_middle_gradient = ADAPTER_SCALE * jnp.einsum(
            "te,re->tr", middle_gradient, output_up_matrix, preferred_element_type=jnp.float32
        )
        output_up_gradient = ADAPTER_SCALE * jnp.einsum(
            "iz,iq->zq", adapter_middle, middle_gradient, preferred_element_type=jnp.float32
        )
        output_down_gradient = exact_product(attention_output.T, adapter_middle_gradient)
        attention_output_gradient = jnp.einsum(
            "te,de->td", middle_gradient, w_out[layer_params], preferred_element_type=jnp.float32
        )
        attention_output_gradient = (
            attention_output_gradient + exact_product(adapter_middle_gradient, output_down_matrix.T)
        ).astype(jnp.bfloat16)
        query_key_value_gradient = attention_back(
            query_key_value, visible, row_lse_l, attention_output_gradient
        )
        qkv_up_gradient = ADAPTER_SCALE * jnp.einsum(
            "iz,iq->zq", adapter_input, query_key_value_gradient, preferred_element_type=jnp.float32
        )
        adapter_input_gradient = ADAPTER_SCALE * jnp.einsum(
            "te,re->tr", query_key_value_gradient, qkv_up_matrix, preferred_element_type=jnp.float32
        )
        qkv_down_gradient = exact_product(hidden_first.T, adapter_input_gradient)
        layer_grads.insert(
            0,
            jnp.concatenate(
                [
                    qkv_down_gradient.reshape(-1),
                    output_down_gradient.reshape(-1),
                    qkv_up_gradient.reshape(-1),
                    output_up_gradient.reshape(-1),
                ]
            ),
        )
    local_grads = jnp.stack(layer_grads)
    grad_shard = lax.psum_scatter(local_grads, "vocab", scatter_dimension=1, tiled=True)
    grad_shard, loss_sum = lax.psum((grad_shard, loss_part), "dp")
    square_sum = lax.psum(jnp.sum(grad_shard * grad_shard), "vocab")
    loss = loss_sum / total_tokens
    grad_norm = jnp.sqrt(square_sum)
    clipped = grad_shard * jnp.minimum(1.0, CLIP_NORM / (grad_norm + 1e-06))
    step = step_count[0].astype(jnp.float32)
    new_first = BETA_ONE * first_moment + (1.0 - BETA_ONE) * clipped
    new_second = BETA_TWO * second_moment + (1.0 - BETA_TWO) * clipped * clipped
    fix_one = 1.0 - jnp.power(BETA_ONE, step)
    fix_two = 1.0 - jnp.power(BETA_TWO, step)
    motion = (
        new_first / fix_one / (jnp.sqrt(new_second / fix_two) + ADAM_EPS) + WEIGHT_DECAY * adapters
    )
    new_adapters = adapters - LEARN_RATE * motion
    return (loss, grad_norm, new_adapters, new_first, new_second, new_adapters.astype(jnp.bfloat16))


def solution(mesh):
    in_specs = (
        P(("vocab", "dp")),
        P(("vocab", "dp")),
        P(("vocab", "dp")),
        P(("vocab", "dp")),
        P("vocab", None),
        P(),
        P(),
        P(),
        P(),
        P(),
        P(),
        P(),
        P(),
        P(None, "vocab"),
        P(None, "vocab"),
        P(None, "vocab"),
        P(),
    )
    out_specs = (P(), P(), P(None, "vocab"), P(None, "vocab"), P(None, "vocab"), P(None, "vocab"))
    return jax.shard_map(local, mesh=mesh, in_specs=in_specs, out_specs=out_specs, check_vma=False)
```

profile of v0, /device:TPU:0, one launch (start us, length us, event | category | flops | bytes accessed | tf_op | source)
XLA Modules:
  0.0 552.6 jit_solution(14179724216567743253)
XLA Ops:
  7.2 10.7 %all-gather.1 = s32[8,1,256]{2,1,0:T(1,128)S(1)} all-gather(s32[1,1,256]{2,1,0:T(1,128)} %bitcast.172), channel_id=1, replica_groups=mesh['vocab'=8,'dp'=4] {'vocab'}, dimensions={0}, use_global_device_ids=true | all-gather | bytes 9216 | tf_op jit(solution)/shard_map/all_gather | solution.py:149
  18.0 17.3 %gather_fusion = bf16[2048,1024]{1,0:T(8,128)(2,1)} fusion(bf16[6288,1024]{1,0:T(8,128)(2,1)} %param.21, s32[2048]{0:T(1024)S(1)} %fusion.86), kind=kCustom, calls=%fused_computation | custom fusion | bytes 8396800 | tf_op jit(solution)/shard_map/jit(_take)/gather | solution.py:156
  35.3 4.1 select_convert_fusion
  40.7 9.5 %all_gather.17 = bf16[1,24576]{1,0:T(2,128)(2,1)S(1)} all-gather(bf16[1,3072]{1,0:T(2,128)(2,1)S(1)} %convert_element_type.95), channel_id=1, replica_groups=mesh['vocab'=8,'dp'=4] {'vocab'}, dimensions={1}, use_global_device_ids=true | all-gather | bytes 55296 | tf_op jit(solution)/shard_map/all_gather | solution.py:163
  51.9 3.5 gather_fusion.1
  55.7 35.3 %reduce-scatter.6.cloned.1.call-done = bf16[256,1024]{1,0:T(8,128)(2,1)} async-done(((bf16[2048,1024]{1,0:T(8,128)(2,1)}), bf16[256,1024]{1,0:T(8,128)(2,1)}) %reduce-scatter.6.cloned.1.call-update) | async-done | bytes 524304 | tf_op jit(solution)/shard_map/reduce_scatter | solution.py:157
  95.1 4.6 fusion.27
  102.9 2.2 copy.46
  105.1 2.0 copy.45
  107.1 1.9 select_reduce_fusion.1
  113.1 1.6 slice-done.5
  114.7 2.6 fusion.17
  117.4 2.8 fusion.112
  121.7 8.9 %all-gather = s32[8,1,256]{2,1,0:T(1,128)S(1)} all-gather(s32[1,1,256]{2,1,0:T(1,128)S(1)} %bitcast.173), channel_id=1, replica_groups=mesh['vocab'=8,'dp'=4] {'vocab'}, dimensions={0}, use_global_device_ids=true | all-gather | bytes 9216 | tf_op jit(solution)/shard_map/all_gather | solution.py:151
  130.6 8.1 %all-gather.2 = s32[8,1,256]{2,1,0:T(1,128)S(1)} all-gather(s32[1,1,256]{2,1,0:T(1,128)S(1)} %bitcast.174), channel_id=1, replica_groups=mesh['vocab'=8,'dp'=4] {'vocab'}, dimensions={0}, use_global_device_ids=true | all-gather | bytes 9216 | tf_op jit(solution)/shard_map/all_gather | solution.py:150
  138.7 19.6 %all-gather.5.cloned.1.call-done = bf16[2048,1024]{1,0:T(8,128)(2,1)} async-done(((bf16[256,1024]{1,0:T(8,128)(2,1)}), bf16[2048,1024]{1,0:T(8,128)(2,1)}) %all-gather.5.cloned.1.call-update) | async-done | bytes 4194320 | tf_op jit(solution)/shard_map/all_gather | solution.py:226
  158.3 35.7 %select_reduce_fusion = (f32[2048]{0:T(1024)S(1)}, f32[2048,6288]{0,1:T(8,128)}) fusion(pred[6288]{0:T(1024)(128)(4,1)S(1)} %broadcast_compare_fusion, bf16[2048,1024]{1,0:T(8,128)(2,1)} %all-gather.5.cloned.1.call-done, bf16[6288,1024]{1,0:T(8,128)(2,1)} %param.21), kind=kOutput, calls=%fused_computation.10 | convolution fusion | flops 26399537152 | bytes 68597904 | tf_op jit(solution)/shard_map/td,vd->tv/dot_general | solution.py:223
  194.1 13.3 %pmax.7 = f32[2048]{0:T(1024)S(1)} all-reduce(f32[2048]{0:T(1024)S(1)} %get-tuple-element.38), channel_id=1, replica_groups=mesh['vocab'=8,'dp'=4] {'vocab'}, use_global_device_ids=true, to_apply=%region_12.13 | all-reduce | flops 2048 | bytes 16384 | tf_op jit(solution)/shard_map/pmax | solution.py:233
  207.4 20.5 %fusion = (f32[2048]{0:T(1024)S(1)}, f32[2048]{0:T(1024)S(1)}) fusion(f32[2048,6288]{0,1:T(8,128)} %get-tuple-element.39, s32[2048]{0:T(1024)S(1)} %bitcast.159, s32[6288]{0:T(1024)S(1)} %iota_add_fusion, pred[6288]{0:T(1024)(128)(4,1)S(1)} %broadcast_compare_fusion, f32[2048]{0:T(1024)S(1)} %get-tuple-element.38), kind=kLoop, calls=%fused_computation.4 | loop fusion | flops 77262848 | bytes 51575504 | tf_op jit(solution)/shard_map/reduce_sum | solution.py:231
  227.9 12.3 %psum.35 = f32[2048]{0:T(1024)S(1)} all-reduce(f32[2048]{0:T(1024)S(1)} %exponential_multiply_fusion), channel_id=1, replica_groups=mesh['vocab'=8,'dp'=4] {'vocab'}, use_global_device_ids=true, to_apply=%region_14.15 | all-reduce | flops 2048 | bytes 16384 | tf_op jit(solution)/shard_map/psum | solution.py:235
  240.2 52.9 %fusion.5 = f32[2048,1024]{1,0:T(8,128)} fusion(bf16[6288,1024]{1,0:T(8,128)(2,1)} %param.21, f32[2048,6288]{0,1:T(8,128)} %get-tuple-element.39, f32[2048]{0:T(1024)S(1)} %log_add_fusion.1, f32[2048]{0:T(1024)S(1)} %bitcast.161, s32[2048]{0:T(1024)S(1)} %bitcast.160, s32[6288]{0:T(1024)S(1)} %iota_add_fusion, pred[6288]{0:T(1024)(128)(4,1)S(1)} %broadcast_compare_fusion), kind=kOutput, calls=%fused_computation.11 | convolution fusion | flops 26476806144 | bytes 72833744 | tf_op jit(solution)/shard_map/dot_general | solution.py:25
  293.2 71.7 %reduce-scatter.8.cloned.1.call-done = f32[256,1024]{1,0:T(8,128)} async-done(((f32[2048,1024]{1,0:T(8,128)}), f32[256,1024]{1,0:T(8,128)}) %reduce-scatter.8.cloned.1.call-update) | async-done | bytes 1048592 | tf_op jit(solution)/shard_map/reduce_scatter | solution.py:245
  364.9 1.5 multiply_reduce_fusion.6
  366.5 14.4 %fusion.104 = (f32[256]{0:T(256)S(1)}, f32[256]{0:T(256)S(1)}, f32[256,1024]{1,0:T(8,128)}) fusion(f32[256]{0:T(256)S(1)} %add_rsqrt_fusion.1, f32[256,1024]{1,0:T(8,128)} %copy-done.3, f32[256]{0:T(256)S(1)} %broadcast_multiply_fusion.5, f32[1024]{0:T(1024)S(1)} %bitcast.169, bf16[1,1024,4096]{2,1,0:T(8,128)(2,1)} %param.28, f32[256,4096]{1,0:T(8,128)} %copy-done.33, ...), kind=kOutput, calls=%fused_computation.162 | convolution fusion | flops 4323803136 | bytes 25182208 | tf_op jit(solution)/shard_map/tf,df->td/dot_general | solution.py:272
  380.9 2.5 add_convert_fusion
  388.7 3.2 fusion.72
  398.4 6.8 %copy.61 = f32[1,24576]{0,1:T(8,128)} copy(f32[1,24576]{1,0:T(1,128)S(1)} %bitcast.147) | data formatting | bytes 196608
  405.9 91.7 %reduce-scatter.10.cloned.1.call-done = f32[3072,1]{1,0:T(8,128)} async-done(((f32[24576,1]{1,0:T(8,128)}), f32[3072,1]{1,0:T(8,128)}) %reduce-scatter.10.cloned.1.call-update) | async-done | bytes 12304
  497.6 1.9 copy.62
  499.5 18.7 %psum.38 = f32[1,3072]{1,0:T(1,128)S(1)} all-reduce(f32[1,3072]{1,0:T(1,128)S(1)} %copy.62), channel_id=1, replica_groups=mesh['vocab'=8,'dp'=4] {'dp'}, use_global_device_ids=true, to_apply=%region_26.27 | all-reduce | flops 3072 | bytes 24576 | tf_op jit(solution)/shard_map/psum | solution.py:315
  518.8 13.0 %all-reduce = (f32[2048]{0:T(1024)S(1)}, f32[]{:T(128)}) all-reduce(f32[2048]{0:T(1024)S(1)} %get-tuple-element.6, f32[]{:T(128)} %multiply_reduce_fusion.7), channel_id=1, replica_groups=mesh['vocab'=8,'dp'=4] {'vocab'}, use_global_device_ids=true, to_apply=%region_16.17 | all-reduce | flops 2049 | bytes 16392 | tf_op jit(solution)/shard_map/psum | solution.py:235
  533.1 9.0 %psum.37 = f32[]{:T(128)} all-reduce(f32[]{:T(128)} %multiply_reduce_fusion.8), channel_id=1, replica_groups=mesh['vocab'=8,'dp'=4] {'dp'}, use_global_device_ids=true, to_apply=%region_18.19 | all-reduce | flops 1 | bytes 8 | tf_op jit(solution)/shard_map/psum | solution.py:315
  (165 shorter events, 29.3 us)
Async XLA Ops:
  7.2 104.3 %copy-start = (bf16[1,1024,1024]{2,1,0:T(8,128)(2,1)S(1)}, bf16[1,1024,1024]{2,1,0:T(8,128)(2,1)}, u32[]{:S(2)}) copy-start(bf16[1,1024,1024]{2,1,0:T(8,128)(2,1)} %param.27) | copy-start | bytes 6291460
  7.2 83.8 %reduce-scatter.6.cloned.1.call-start = ((), (), s32[]{:S(2)}) async-start(), calls=%async_computation.3 | async-start | bytes 4718592 | tf_op jit(solution)/shard_map/reduce_scatter | solution.py:157
  39.4 16.0 %copy-start.23 = (f32[1,9216]{1,0:T(1,128)S(1)}, f32[1,9216]{1,0:T(1,128)}, u32[]{:S(2)}) copy-start(f32[1,9216]{1,0:T(1,128)} %param.25) | copy-start | bytes 110596
  39.4 16.1 %copy-start.27 = (f32[3,1024]{1,0:T(4,128)S(1)}, f32[3,1024]{1,0:T(4,128)}, u32[]{:S(2)}) copy-start(f32[3,1024]{1,0:T(4,128)} %param.23) | copy-start | bytes 36868
  39.4 16.1 %copy-start.28 = (f32[3,1024]{1,0:T(4,128)S(1)}, f32[3,1024]{1,0:T(4,128)}, u32[]{:S(2)}) copy-start(f32[3,1024]{1,0:T(4,128)} %param.24) | copy-start | bytes 36868
  39.5 118.9 %all-gather.5.cloned.1.call-start = ((), (), s32[]{:S(2)}) async-start(), calls=%async_computation.4 | async-start | bytes 4718592 | tf_op jit(solution)/shard_map/all_gather | solution.py:226
  50.4 49.4 %copy-start.19 = (bf16[4,3072]{1,0:T(4,128)(2,1)}, bf16[4,3072]{1,0:T(4,128)(2,1)S(1)}, u32[]{:S(2)}) copy-start(bf16[4,3072]{1,0:T(4,128)(2,1)S(1)} %reshape.265) | copy-start | bytes 73732
  51.1 60.1 %copy-start.12 = (bf16[1024,4]{1,0:T(8,128)(2,1)}, bf16[1024,4]{1,0:T(8,128)(2,1)S(1)}, u32[]{:S(2)}) copy-start(bf16[1024,4]{1,0:T(8,128)(2,1)S(1)} %reshape.269) | copy-start | bytes 24580
  51.9 43.2 %slice-start = ((f32[1,9216]{1,0:T(1,128)}), f32[1,3072]{1,0:T(1,128)S(1)}, s32[]{:S(2)}) async-start(f32[1,9216]{1,0:T(1,128)} %param.25), calls=%async_computation.7 | async-start | bytes 24576 | tf_op jit(solution)/shard_map/slice | solution.py:179
  55.7 54.3 %copy-start.17 = (pred[256,256]{0,1:T(8,128)(4,1)}, pred[256,256]{0,1:T(8,128)(4,1)S(1)}, u32[]{:S(2)}) copy-start(pred[256,256]{0,1:T(8,128)(4,1)S(1)} %fusion.84) | copy-start | bytes 196612
  94.9 4.9 copy-start.7
  95.1 4.7 copy-start.29
  102.9 7.1 %copy-start.9 = (bf16[256,1024]{0,1:T(8,128)(2,1)}, bf16[256,1024]{0,1:T(8,128)(2,1)S(1)}, u32[]{:S(2)}) copy-start(bf16[256,1024]{0,1:T(8,128)(2,1)S(1)} %copy.47) | copy-start | bytes 1572868
  107.1 2.9 copy-start.14
  110.0 3.1 slice-start.4
  110.0 4.7 slice-start.5
  111.3 3.4 slice-start.1
  112.3 5.1 slice-start.2
  112.8 4.6 copy-start.3
  117.3 2.9 copy-start.33
  117.4 4.3 copy-start.31
  117.4 13.2 %copy-start.32 = (s32[256]{0:T(256)S(1)}, s32[256]{0:T(256)}, u32[]{:S(2)}) copy-start(s32[256]{0:T(256)} %param.18) | copy-start | bytes 3076
  121.6 243.3 %reduce-scatter.8.cloned.1.call-start = ((), (), s32[]{:S(2)}) async-start(), calls=%async_computation.5 | async-start | bytes 9437184 | tf_op jit(solution)/shard_map/reduce_scatter | solution.py:245
  293.1 204.5 %reduce-scatter.10.cloned.1.call-start = ((), (), s32[]{:S(2)}) async-start(), calls=%async_computation.6 | async-start | bytes 14155776
  380.9 3.7 copy-start.6
  380.9 5.1 copy-start.13
  383.6 5.1 copy-start.18
  386.0 6.0 %copy-start.15 = (bf16[256,1024]{0,1:T(8,128)(2,1)S(1)}, bf16[256,1024]{0,1:T(8,128)(2,1)}, u32[]{:S(2)}) copy-start(bf16[256,1024]{0,1:T(8,128)(2,1)} %copy.45) | copy-start | bytes 1572868
  388.7 3.5 copy-start.2
  405.1 137.7 %copy-start.22 = (f32[1,3072]{1,0:T(1,128)S(1)}, f32[1,3072]{1,0:T(1,128)}, u32[]{:S(2)}) copy-start(f32[1,3072]{1,0:T(1,128)} %param.30) | copy-start | bytes 36868
  405.1 137.7 %copy-start.25 = (f32[1,3072]{1,0:T(1,128)S(1)}, f32[1,3072]{1,0:T(1,128)}, u32[]{:S(2)}) copy-start(f32[1,3072]{1,0:T(1,128)} %param.32) | copy-start | bytes 36868
  405.1 137.7 %copy-start.26 = (f32[1,3072]{1,0:T(1,128)S(1)}, f32[1,3072]{1,0:T(1,128)}, u32[]{:S(2)}) copy-start(f32[1,3072]{1,0:T(1,128)} %param.31) | copy-start | bytes 36868
  (12 other events, 17.8 us)
Sparse Core Ops, SparseCore 0:
  39.6 51.2 reduce-scatter.5
  121.7 36.5 all-gather.4
  293.3 71.5 reduce-scatter.7
  405.3 92.2 reduce-scatter.9
where the time goes:
time: 557 us; the launch traced here: 553 us
  waiting for transfers between devices  218 us (39%)
  matrix products  130 us (23%)
  blocking collectives  104 us (19%)
  local copies, waits for them, and re-layouts  42.4 us (8%)
  other arithmetic  39 us (7%)
  between operations  19.2 us (3%)
    unnamed x5, waiting for transfers between devices  91.8 us
    reduce_scatter x1, waiting for transfers between devices, local(): lax.psum_scatter(mixed_product(grad_logits, embed_table), 'vocab', scatte...  71.7 us
    dot_general x9, matrix products, mixed_product(): return jnp.dot(left, right, preferred_element_type=jnp.float32)  65.3 us
    dot_general x1, matrix products, head_logits(): jnp.einsum('td,vd->tv', row_block, embed_table, preferred_element_type=jn...  35.7 us
    reduce_scatter x1, waiting for transfers between devices, local(): lax.psum_scatter(jnp.where(inside[:, None], picked_rows.astype(jnp.float3...  35.3 us
    psum x2, blocking collectives, local(): grad_shard, loss_sum = lax.psum((grad_shard, loss_part), 'dp')  27.7 us
    psum x2, blocking collectives, local(): row_total, picked = lax.psum((row_total, picked), 'vocab')  25.3 us
    reduce_sum x1, other arithmetic, local(): jnp.sum(jnp.where(columns[None, :] == wanted[:, None], logits, 0.0), -1)  20.5 us
  transfers between devices with their start and end apart: 4, of which 4 were waited for; matrix products, arithmetic and copies ran while one was open for 1% of the time, Pallas kernels for 0%

commit v1 on v0

--- a/solution.py
+++ b/solution.py
@@ -223,7 +223,30 @@
         logits = jnp.einsum("td,vd->tv", row_block, embed_table, preferred_element_type=jnp.float32)
         return jnp.where(live[None], logits, -1e30)
 
-    piece = lax.all_gather(hidden, "vocab", axis=0, tiled=True)
+    seen_now, tall, then = (lax.axis_size("vocab"), lax.axis_index("vocab"), hidden.shape[0])
+    fields = []
+    for no, at in enumerate(hidden.shape):
+        fields.append(at * seen_now if no == 0 else at)
+    piece = lax.dynamic_update_slice_in_dim(
+        jnp.zeros(fields, hidden.dtype), hidden, tall * then, axis=0
+    )
+    earlier = state_next = hidden
+    for m in range(1, seen_now // 2 + 1):
+        runs = []
+        for no in range(seen_now):
+            runs.append((no, (no + 1) % seen_now))
+        earlier = lax.ppermute(earlier, "vocab", perm=runs)
+        piece = lax.dynamic_update_slice_in_dim(
+            piece, earlier, (tall - m) % seen_now * then, axis=0
+        )
+        if 2 * m < seen_now:
+            gallery = []
+            for no in range(seen_now):
+                gallery.append((no, (no - 1) % seen_now))
+            state_next = lax.ppermute(state_next, axis_name="vocab", perm=gallery)
+            piece = lax.dynamic_update_slice_in_dim(
+                piece, state_next, (tall + m) % seen_now * then, axis=0
+            )
     logits = head_logits(piece)
     row_top = jnp.max(logits, -1)
     row_total = jnp.sum(jnp.exp(logits - row_top[:, None]), -1)

time: 557 us -> 587 us (1.054)
  local copies, waits for them, and re-layouts: 42.4 us -> 56.9 us
  waiting for transfers between devices: 218 us -> 225 us
  starting transfers between devices: 0.16 us -> 6.89 us
    ppermute x0 -> x7, waiting for transfers between devices: none -> 27.3 us  [the longest x4 26 us: local(): earlier = lax.ppermute(earlier, 'vocab', perm=runs)]
    all_gather x1 -> x0, waiting for transfers between devices: 19.6 us -> none  [local(): piece = lax.all_gather(hidden, 'vocab', axis=0, tiled=True)]
    dynamic_update_slice x0 -> x7, local copies, waits for them, and re-layouts: none -> 11.1 us  [the longest x4 6.51 us: local(): lax.dynamic_update_slice_in_dim(piece, earlier, (tall - m) % seen_now * t...]
    ppermute x0 -> x7, starting transfers between devices: none -> 6.76 us  [the longest x3 6.75 us: local(): state_next = lax.ppermute(state_next, axis_name='vocab', perm=gallery)]
    unnamed x80 -> x86, local copies, waits for them, and re-layouts: 11.5 us -> 12.3 us
    unnamed x5 -> x4, waiting for transfers between devices: 91.8 us -> 91.7 us
  transfers between devices with their start and end apart: 4 -> 10, of which waited for: 4 -> 7; matrix products, arithmetic and copies ran while one was open for 1% -> 3% of each run, Pallas kernels for 0% -> 0%
where the time goes in v1:
time: 587 us; the launch traced here: 583 us
  waiting for transfers between devices  225 us (38%)
  matrix products  130 us (22%)
  blocking collectives  106 us (18%)
  local copies, waits for them, and re-layouts  56.9 us (10%)
  other arithmetic  39 us (7%)
  between operations  19.3 us (3%)
  starting transfers between devices  6.89 us (1%)
    unnamed x4, waiting for transfers between devices  91.7 us
    reduce_scatter x1, waiting for transfers between devices, local(): lax.psum_scatter(mixed_product(grad_logits, embed_table), 'vocab', scatte...  70.9 us
    dot_general x9, matrix products, mixed_product(): return jnp.dot(left, right, preferred_element_type=jnp.float32)  65.3 us
    dot_general x1, matrix products, head_logits(): jnp.einsum('td,vd->tv', row_block, embed_table, preferred_element_type=jn...  35.7 us
    reduce_scatter x1, waiting for transfers between devices, local(): lax.psum_scatter(jnp.where(inside[:, None], picked_rows.astype(jnp.float3...  35.3 us
    psum x2, blocking collectives, local(): grad_shard, loss_sum = lax.psum((grad_shard, loss_part), 'dp')  27.7 us
    ppermute x4, waiting for transfers between devices, local(): earlier = lax.ppermute(earlier, 'vocab', perm=runs)  26 us
    psum x2, blocking collectives, local(): row_total, picked = lax.psum((row_total, picked), 'vocab')  25.3 us
  transfers between devices with their start and end apart: 10, of which 7 were waited for; matrix products, arithmetic and copies ran while one was open for 3% of the time, Pallas kernels for 0%

profile of v1, /device:TPU:0, one launch (start us, length us, event | category | flops | bytes accessed | tf_op | source)
XLA Modules:
  0.0 582.7 jit_solution(2534361294629523034)
XLA Ops:
  7.2 10.7 %all-gather.1 = s32[8,1,256]{2,1,0:T(1,128)S(1)} all-gather(s32[1,1,256]{2,1,0:T(1,128)} %bitcast.172), channel_id=1, replica_groups=mesh['vocab'=8,'dp'=4] {'vocab'}, dimensions={0}, use_global_device_ids=true | all-gather | bytes 9216 | tf_op jit(solution)/shard_map/all_gather | solution.py:149
  18.0 17.3 %gather_fusion = bf16[2048,1024]{1,0:T(8,128)(2,1)} fusion(bf16[6288,1024]{1,0:T(8,128)(2,1)} %param.21, s32[2048]{0:T(1024)S(1)} %fusion.86), kind=kCustom, calls=%fused_computation | custom fusion | bytes 8396800 | tf_op jit(solution)/shard_map/jit(_take)/gather | solution.py:156
  35.3 4.1 select_convert_fusion
  40.7 9.5 %all_gather.14 = bf16[1,24576]{1,0:T(2,128)(2,1)S(1)} all-gather(bf16[1,3072]{1,0:T(2,128)(2,1)S(1)} %convert_element_type.95), channel_id=1, replica_groups=mesh['vocab'=8,'dp'=4] {'vocab'}, dimensions={1}, use_global_device_ids=true | all-gather | bytes 55296 | tf_op jit(solution)/shard_map/all_gather | solution.py:163
  51.9 3.5 gather_fusion.1
  55.7 35.3 %reduce-scatter.6.cloned.1.call-done = bf16[256,1024]{1,0:T(8,128)(2,1)} async-done(((bf16[2048,1024]{1,0:T(8,128)(2,1)}), bf16[256,1024]{1,0:T(8,128)(2,1)}) %reduce-scatter.6.cloned.1.call-update) | async-done | bytes 524304 | tf_op jit(solution)/shard_map/reduce_scatter | solution.py:157
  95.1 4.6 fusion.27
  102.9 2.2 copy.46
  114.7 2.6 fusion.17
  117.4 2.8 fusion.112
  120.5 2.6 broadcast_in_dim.106
  124.2 2.6 collective-permute-start.1
  126.8 11.6 %collective-permute-done = bf16[256,1024]{1,0:T(8,128)(2,1)S(1)} collective-permute-done((bf16[256,1024]{1,0:T(8,128)(2,1)S(1)}, bf16[256,1024]{1,0:T(8,128)(2,1)S(1)}, u32[]{:S(2)}, u32[]{:S(2)}) %collective-permute-start) | collective-permute-done | bytes 524320 | tf_op jit(solution)/shard_map/ppermute | solution.py:238
  139.2 2.6 collective-permute-start.3
  141.9 12.3 %collective-permute-done.2 = bf16[256,1024]{1,0:T(8,128)(2,1)} collective-permute-done((bf16[256,1024]{1,0:T(8,128)(2,1)S(1)}, bf16[256,1024]{1,0:T(8,128)(2,1)}, u32[]{:S(2)}, u32[]{:S(2)}) %collective-permute-start.2) | collective-permute-done | bytes 524320 | tf_op jit(solution)/shard_map/ppermute | solution.py:238
  154.1 10.5 %all-gather = s32[8,1,256]{2,1,0:T(1,128)S(1)} all-gather(s32[1,1,256]{2,1,0:T(1,128)S(1)} %bitcast.173), channel_id=1, replica_groups=mesh['vocab'=8,'dp'=4] {'vocab'}, dimensions={0}, use_global_device_ids=true | all-gather | bytes 9216 | tf_op jit(solution)/shard_map/all_gather | solution.py:151
  164.7 9.2 %all-gather.2 = s32[8,1,256]{2,1,0:T(1,128)S(1)} all-gather(s32[1,1,256]{2,1,0:T(1,128)S(1)} %bitcast.174), channel_id=1, replica_groups=mesh['vocab'=8,'dp'=4] {'vocab'}, dimensions={0}, use_global_device_ids=true | all-gather | bytes 9216 | tf_op jit(solution)/shard_map/all_gather | solution.py:150
  187.0 2.2 collective-permute-done.6
  190.0 35.7 %select_reduce_fusion = (f32[2048]{0:T(1024)S(1)}, f32[2048,6288]{0,1:T(8,128)}) fusion(pred[6288]{0:T(1024)(128)(4,1)S(1)} %broadcast_compare_fusion, bf16[2048,1024]{1,0:T(8,128)(2,1)} %constant_dynamic-update-slice_fusion, bf16[6288,1024]{1,0:T(8,128)(2,1)} %param.21), kind=kOutput, calls=%fused_computation.10 | convolution fusion | flops 26399537152 | bytes 68597904 | tf_op jit(solution)/shard_map/td,vd->tv/dot_general | solution.py:223
  225.7 12.6 %pmax.7 = f32[2048]{0:T(1024)S(1)} all-reduce(f32[2048]{0:T(1024)S(1)} %get-tuple-element.40), channel_id=1, replica_groups=mesh['vocab'=8,'dp'=4] {'vocab'}, use_global_device_ids=true, to_apply=%region_12.13 | all-reduce | flops 2048 | bytes 16384 | tf_op jit(solution)/shard_map/pmax | solution.py:256
  238.3 20.5 %fusion = (f32[2048]{0:T(1024)S(1)}, f32[2048]{0:T(1024)S(1)}) fusion(f32[2048,6288]{0,1:T(8,128)} %get-tuple-element.41, s32[2048]{0:T(1024)S(1)} %bitcast.159, s32[6288]{0:T(1024)S(1)} %iota_add_fusion, pred[6288]{0:T(1024)(128)(4,1)S(1)} %broadcast_compare_fusion, f32[2048]{0:T(1024)S(1)} %get-tuple-element.40), kind=kLoop, calls=%fused_computation.4 | loop fusion | flops 77262848 | bytes 51575504 | tf_op jit(solution)/shard_map/reduce_sum | solution.py:254
  258.8 12.3 %psum.35 = f32[2048]{0:T(1024)S(1)} all-reduce(f32[2048]{0:T(1024)S(1)} %exponential_multiply_fusion), channel_id=1, replica_groups=mesh['vocab'=8,'dp'=4] {'vocab'}, use_global_device_ids=true, to_apply=%region_14.15 | all-reduce | flops 2048 | bytes 16384 | tf_op jit(solution)/shard_map/psum | solution.py:258
  271.1 53.0 %fusion.5 = f32[2048,1024]{1,0:T(8,128)} fusion(bf16[6288,1024]{1,0:T(8,128)(2,1)} %param.21, f32[2048,6288]{0,1:T(8,128)} %get-tuple-element.41, f32[2048]{0:T(1024)S(1)} %log_add_fusion.1, f32[2048]{0:T(1024)S(1)} %bitcast.161, s32[2048]{0:T(1024)S(1)} %bitcast.160, s32[6288]{0:T(1024)S(1)} %iota_add_fusion, pred[6288]{0:T(1024)(128)(4,1)S(1)} %broadcast_compare_fusion), kind=kOutput, calls=%fused_computation.11 | convolution fusion | flops 26476806144 | bytes 72833744 | tf_op jit(solution)/shard_map/dot_general | solution.py:25
  324.2 70.9 %reduce-scatter.8.cloned.1.call-done = f32[256,1024]{1,0:T(8,128)} async-done(((f32[2048,1024]{1,0:T(8,128)}), f32[256,1024]{1,0:T(8,128)}) %reduce-scatter.8.cloned.1.call-update) | async-done | bytes 1048592 | tf_op jit(solution)/shard_map/reduce_scatter | solution.py:268
  396.6 14.4 %fusion.104 = (f32[256]{0:T(256)S(1)}, f32[256]{0:T(256)S(1)}, f32[256,1024]{1,0:T(8,128)}) fusion(f32[256]{0:T(256)S(1)} %add_rsqrt_fusion.1, f32[256,1024]{1,0:T(8,128)} %copy-done.3, f32[256]{0:T(256)S(1)} %broadcast_multiply_fusion.5, f32[1024]{0:T(1024)S(1)} %bitcast.169, bf16[1,1024,4096]{2,1,0:T(8,128)(2,1)} %param.28, f32[256,4096]{1,0:T(8,128)} %copy-done.36, ...), kind=kOutput, calls=%fused_computation.170 | convolution fusion | flops 4323803136 | bytes 25182208 | tf_op jit(solution)/shard_map/tf,df->td/dot_general | solution.py:295
  411.0 2.5 add_convert_fusion
  418.9 3.2 fusion.72
  428.5 6.8 %copy.61 = f32[1,24576]{0,1:T(8,128)} copy(f32[1,24576]{1,0:T(1,128)S(1)} %bitcast.147) | data formatting | bytes 196608
  436.0 91.7 %reduce-scatter.10.cloned.1.call-done = f32[3072,1]{1,0:T(8,128)} async-done(((f32[24576,1]{1,0:T(8,128)}), f32[3072,1]{1,0:T(8,128)}) %reduce-scatter.10.cloned.1.call-update) | async-done | bytes 12304
  529.6 18.7 %psum.38 = f32[1,3072]{1,0:T(1,128)S(1)} all-reduce(f32[1,3072]{1,0:T(1,128)S(1)} %copy.62), channel_id=1, replica_groups=mesh['vocab'=8,'dp'=4] {'dp'}, use_global_device_ids=true, to_apply=%region_26.27 | all-reduce | flops 3072 | bytes 24576 | tf_op jit(solution)/shard_map/psum | solution.py:338
  548.9 13.0 %all-reduce = (f32[2048]{0:T(1024)S(1)}, f32[]{:T(128)}) all-reduce(f32[2048]{0:T(1024)S(1)} %get-tuple-element.6, f32[]{:T(128)} %multiply_reduce_fusion.7), channel_id=1, replica_groups=mesh['vocab'=8,'dp'=4] {'vocab'}, use_global_device_ids=true, to_apply=%region_16.17 | all-reduce | flops 2049 | bytes 16392 | tf_op jit(solution)/shard_map/psum | solution.py:258
  563.2 9.0 %psum.37 = f32[]{:T(128)} all-reduce(f32[]{:T(128)} %multiply_reduce_fusion.8), channel_id=1, replica_groups=mesh['vocab'=8,'dp'=4] {'dp'}, use_global_device_ids=true, to_apply=%region_18.19 | all-reduce | flops 1 | bytes 8 | tf_op jit(solution)/shard_map/psum | solution.py:338
  (190 shorter events, 52.9 us)
Async XLA Ops:
  7.2 104.3 %copy-start = (bf16[1,1024,1024]{2,1,0:T(8,128)(2,1)S(1)}, bf16[1,1024,1024]{2,1,0:T(8,128)(2,1)}, u32[]{:S(2)}) copy-start(bf16[1,1024,1024]{2,1,0:T(8,128)(2,1)} %param.27) | copy-start | bytes 6291460
  7.2 83.8 %reduce-scatter.6.cloned.1.call-start = ((), (), s32[]{:S(2)}) async-start(), calls=%async_computation.3 | async-start | bytes 4718592 | tf_op jit(solution)/shard_map/reduce_scatter | solution.py:157
  39.4 16.0 %copy-start.24 = (f32[1,9216]{1,0:T(1,128)S(1)}, f32[1,9216]{1,0:T(1,128)}, u32[]{:S(2)}) copy-start(f32[1,9216]{1,0:T(1,128)} %param.25) | copy-start | bytes 110596
  39.4 16.1 %copy-start.30 = (f32[3,1024]{1,0:T(4,128)S(1)}, f32[3,1024]{1,0:T(4,128)}, u32[]{:S(2)}) copy-start(f32[3,1024]{1,0:T(4,128)} %param.23) | copy-start | bytes 36868
  39.4 16.1 %copy-start.31 = (f32[3,1024]{1,0:T(4,128)S(1)}, f32[3,1024]{1,0:T(4,128)}, u32[]{:S(2)}) copy-start(f32[3,1024]{1,0:T(4,128)} %param.24) | copy-start | bytes 36868
  39.5 355.6 %reduce-scatter.8.cloned.1.call-start = ((), (), s32[]{:S(2)}) async-start(), calls=%async_computation.4 | async-start | bytes 9437184 | tf_op jit(solution)/shard_map/reduce_scatter | solution.py:268
  50.4 49.4 %copy-start.20 = (bf16[4,3072]{1,0:T(4,128)(2,1)}, bf16[4,3072]{1,0:T(4,128)(2,1)S(1)}, u32[]{:S(2)}) copy-start(bf16[4,3072]{1,0:T(4,128)(2,1)S(1)} %reshape.265) | copy-start | bytes 73732
  51.1 60.1 %copy-start.12 = (bf16[1024,4]{1,0:T(8,128)(2,1)}, bf16[1024,4]{1,0:T(8,128)(2,1)S(1)}, u32[]{:S(2)}) copy-start(bf16[1024,4]{1,0:T(8,128)(2,1)S(1)} %reshape.269) | copy-start | bytes 24580
  51.9 43.2 %slice-start = ((f32[1,9216]{1,0:T(1,128)}), f32[1,3072]{1,0:T(1,128)S(1)}, s32[]{:S(2)}) async-start(f32[1,9216]{1,0:T(1,128)} %param.25), calls=%async_computation.6 | async-start | bytes 24576 | tf_op jit(solution)/shard_map/slice | solution.py:179
  55.7 54.3 %copy-start.17 = (pred[256,256]{0,1:T(8,128)(4,1)}, pred[256,256]{0,1:T(8,128)(4,1)S(1)}, u32[]{:S(2)}) copy-start(pred[256,256]{0,1:T(8,128)(4,1)S(1)} %fusion.84) | copy-start | bytes 196612
  94.9 4.9 copy-start.7
  95.1 4.7 copy-start.32
  102.9 7.1 %copy-start.9 = (bf16[256,1024]{0,1:T(8,128)(2,1)}, bf16[256,1024]{0,1:T(8,128)(2,1)S(1)}, u32[]{:S(2)}) copy-start(bf16[256,1024]{0,1:T(8,128)(2,1)S(1)} %copy.47) | copy-start | bytes 1572868
  110.0 4.7 slice-start.5
  111.5 5.8 %copy-start.25 = (bf16[256,4]{0,1:T(4,128)(2,1)}, bf16[256,4]{0,1:T(4,128)(2,1)S(1)}, u32[]{:S(2)}) copy-start(bf16[256,4]{0,1:T(4,128)(2,1)S(1)} %convolution_convert_fusion) | copy-start | bytes 6148
  112.3 5.1 slice-start.2
  120.2 33.9 %copy-start.34 = (s32[256]{0:T(256)S(1)}, s32[256]{0:T(256)}, u32[]{:S(2)}) copy-start(s32[256]{0:T(256)} %param.19) | copy-start | bytes 3076
  120.2 44.4 %copy-start.35 = (s32[256]{0:T(256)S(1)}, s32[256]{0:T(256)}, u32[]{:S(2)}) copy-start(s32[256]{0:T(256)} %param.18) | copy-start | bytes 3076
  124.2 14.2 %collective-permute-start = (bf16[256,1024]{1,0:T(8,128)(2,1)S(1)}, bf16[256,1024]{1,0:T(8,128)(2,1)S(1)}, u32[]{:S(2)}, u32[]{:S(2)}) collective-permute-start(bf16[256,1024]{1,0:T(8,128)(2,1)S(1)} %get-tuple-element.22), channel_id=1, source_target_pairs={{0,4},{4,8},{8,12},{12,16},{16,20},{20,24},{24,28},{28,0},{1,5},{5... | collective-permute-start | bytes 1572872 | tf_op jit(solution)/shard_map/ppermute | solution.py:238
  124.2 15.1 %collective-permute-start.1 = (bf16[256,1024]{1,0:T(8,128)(2,1)S(1)}, bf16[256,1024]{1,0:T(8,128)(2,1)}, u32[]{:S(2)}, u32[]{:S(2)}) collective-permute-start(bf16[256,1024]{1,0:T(8,128)(2,1)S(1)} %get-tuple-element.22), channel_id=1, source_target_pairs={{0,28},{4,0},{8,4},{12,8},{16,12},{20,16},{24,20},{28,24},{1,29},{... | collective-permute-start | bytes 1572872 | tf_op jit(solution)/shard_map/ppermute | solution.py:246
  139.2 14.9 %collective-permute-start.2 = (bf16[256,1024]{1,0:T(8,128)(2,1)S(1)}, bf16[256,1024]{1,0:T(8,128)(2,1)}, u32[]{:S(2)}, u32[]{:S(2)}) collective-permute-start(bf16[256,1024]{1,0:T(8,128)(2,1)S(1)} %collective-permute-done), channel_id=1, source_target_pairs={{0,4},{4,8},{8,12},{12,16},{16,20},{20,24},{24,28},{28,0},{1,5},{5... | collective-permute-start | bytes 1572872 | tf_op jit(solution)/shard_map/ppermute | solution.py:238
  139.2 34.7 %collective-permute-start.3 = (bf16[256,1024]{1,0:T(8,128)(2,1)}, bf16[256,1024]{1,0:T(8,128)(2,1)}, u32[]{:S(2)}, u32[]{:S(2)}) collective-permute-start(bf16[256,1024]{1,0:T(8,128)(2,1)} %collective-permute-done.1), channel_id=1, source_target_pairs={{0,28},{4,0},{8,4},{12,8},{16,12},{20,16},{24,20},{28,24},{1,29},{... | collective-permute-start | bytes 1572872 | tf_op jit(solution)/shard_map/ppermute | solution.py:246
  154.1 23.2 %collective-permute-start.4 = (bf16[256,1024]{1,0:T(8,128)(2,1)}, bf16[256,1024]{1,0:T(8,128)(2,1)}, u32[]{:S(2)}, u32[]{:S(2)}) collective-permute-start(bf16[256,1024]{1,0:T(8,128)(2,1)} %collective-permute-done.2), channel_id=1, source_target_pairs={{0,4},{4,8},{8,12},{12,16},{16,20},{20,24},{24,28},{28,0},{1,5},{5... | collective-permute-start | bytes 1572872 | tf_op jit(solution)/shard_map/ppermute | solution.py:238
  174.0 12.2 %collective-permute-start.5 = (bf16[256,1024]{1,0:T(8,128)(2,1)}, bf16[256,1024]{1,0:T(8,128)(2,1)S(1)}, u32[]{:S(2)}, u32[]{:S(2)}) collective-permute-start(bf16[256,1024]{1,0:T(8,128)(2,1)} %collective-permute-done.3), channel_id=1, source_target_pairs={{0,28},{4,0},{8,4},{12,8},{16,12},{20,16},{24,20},{28,24},{1,29},{... | collective-permute-start | bytes 1572872 | tf_op jit(solution)/shard_map/ppermute | solution.py:246
  177.3 11.8 %collective-permute-start.6 = (bf16[256,1024]{1,0:T(8,128)(2,1)}, bf16[256,1024]{1,0:T(8,128)(2,1)S(1)}, u32[]{:S(2)}, u32[]{:S(2)}) collective-permute-start(bf16[256,1024]{1,0:T(8,128)(2,1)} %collective-permute-done.4), channel_id=1, source_target_pairs={{0,4},{4,8},{8,12},{12,16},{16,20},{20,24},{24,28},{28,0},{1,5},{5... | collective-permute-start | bytes 1572872 | tf_op jit(solution)/shard_map/ppermute | solution.py:238
  324.1 203.6 %reduce-scatter.10.cloned.1.call-start = ((), (), s32[]{:S(2)}) async-start(), calls=%async_computation.5 | async-start | bytes 14155776
  411.0 5.1 copy-start.13
  413.8 5.1 copy-start.18
  416.1 6.0 %copy-start.15 = (bf16[256,1024]{0,1:T(8,128)(2,1)S(1)}, bf16[256,1024]{0,1:T(8,128)(2,1)}, u32[]{:S(2)}) copy-start(bf16[256,1024]{0,1:T(8,128)(2,1)} %copy.45) | copy-start | bytes 1572868
  435.3 137.7 %copy-start.23 = (f32[1,3072]{1,0:T(1,128)S(1)}, f32[1,3072]{1,0:T(1,128)}, u32[]{:S(2)}) copy-start(f32[1,3072]{1,0:T(1,128)} %param.30) | copy-start | bytes 36868
  435.3 137.7 %copy-start.28 = (f32[1,3072]{1,0:T(1,128)S(1)}, f32[1,3072]{1,0:T(1,128)}, u32[]{:S(2)}) copy-start(f32[1,3072]{1,0:T(1,128)} %param.32) | copy-start | bytes 36868
  435.3 137.7 %copy-start.29 = (f32[1,3072]{1,0:T(1,128)S(1)}, f32[1,3072]{1,0:T(1,128)}, u32[]{:S(2)}) copy-start(f32[1,3072]{1,0:T(1,128)} %param.31) | copy-start | bytes 36868
  (21 other events, 45.5 us)
Sparse Core Ops, SparseCore 0:
  39.6 51.2 reduce-scatter.5
  324.2 70.7 reduce-scatter.7
  435.4 92.2 reduce-scatter.9
